TPU v7x, 128 devices: a whole 4x4x4 slice. The times are simulated.
128 devices in a mesh: gx: 16 (over z_lo, x, core), gy: 8 (over y, z_hi).
Axes of the slice: x: 4, y: 4, z: 4 (z_hi: 2, z_lo: 2; z = z_hi * 2 + z_lo), core: 2. Of those that a mesh axis runs over, the one named last changes fastest.
Arguments:
- pair_in: bfloat16 [1024, 1024, 128], P(('gx', 'gy')), may hold values from -6 to 6
- residue_mask: int32 [1024], P(('gx', 'gy')), may hold values 0 or 1
- norm_start: float32 [128], replicated, may hold values from 0.25 to 1.75
- proj_start: bfloat16 [128, 512], replicated, may hold values from -0.5 to 0.5
- gate_bias_start: float32 [128], replicated, may hold values from -4 to 4
- bias_w_start: bfloat16 [128, 4], replicated, may hold values from -1.5 to 1.5
- out_w_start: bfloat16 [128, 128], replicated, may hold values from -1 to 1
- norm_end: float32 [128], replicated, may hold values from 0.25 to 1.75
- proj_end: bfloat16 [128, 512], replicated, may hold values from -0.5 to 0.5
- gate_bias_end: float32 [128], replicated, may hold values from -4 to 4
- bias_w_end: bfloat16 [128, 4], replicated, may hold values from -1.5 to 1.5
- out_w_end: bfloat16 [128, 128], replicated, may hold values from -1 to 1
- norm_trans: float32 [128], replicated, may hold values from 0.25 to 1.75
- trans_in: bfloat16 [128, 512], replicated, may hold values from -0.5 to 0.5
- trans_bias: float32 [512], replicated, may hold values from -4 to 4
- trans_out: bfloat16 [512, 128], replicated, may hold values from -0.375 to 0.375
Outputs:
- pair_out: bfloat16 [1024, 1024, 128], P(('gx', 'gy'))
Inputs may be any that keep to these rules, and one draw needn't show every extreme that they name: residue_mask holds only 0 and 1.
All inputs are finite; a program needn't handle non-finite values.
Results may differ from a plain program's by a relative error of at most 0.02.
Values may be sent and summed in bfloat16 or wider, within the bound.
A program may use at most 192 MiB of HBM per device.

v0:
```python
import functools
import math

import jax
import jax.numpy as jnp
from jax import lax
from jax.experimental import pallas as pl
from jax.experimental.pallas import tpu as pltpu
from jax.sharding import PartitionSpec as P

HEADS = 4
HEAD_DIM = 32
BIG = 1000000000.0
LOG2E = math.log2(math.e)
QSCALE = HEAD_DIM ** (-0.5) * LOG2E
MESH = pl.DeviceIdType.MESH
F32 = jnp.float32
BF16 = jnp.bfloat16


def nn(a, b):
    return lax.dot_general(a, b, (((1,), (0,)), ((), ())), preferred_element_type=F32)


def nt(a, b):
    return lax.dot_general(a, b, (((1,), (1,)), ((), ())), preferred_element_type=F32)


def layer_norm(x, gain):
    mean = jnp.mean(x, axis=-1, keepdims=True)
    cent = x - mean
    var = jnp.mean(cent * cent, axis=-1, keepdims=True)
    return (cent * lax.rsqrt(var + 1e-05) * gain).astype(BF16)


def bias_rows(w, r, rows, normed):
    shape = (HEADS * rows, HEADS)
    place = lax.broadcasted_iota(jnp.int32, shape, 0) == (
        lax.broadcasted_iota(jnp.int32, shape, 1) * rows + r
    )
    spread = nn(place.astype(F32).astype(BF16), w).astype(BF16)
    return nt(spread, normed)


def attend_tile(tq, ck, t, q_ref, k_ref, v_ref, bias_ref, s_refs, finish):
    rows, res, ch = k_ref.shape
    lanes = pl.ds(pl.multiple_of(t * tq, tq), tq)
    chunks = res // ck

    def query(r, h):
        q = q_ref[r, :, lanes]
        row = lax.broadcasted_iota(jnp.int32, q.shape, 0)
        return jnp.where((row >= h * HEAD_DIM) & (row < (h + 1) * HEAD_DIM), q, jnp.zeros_like(q))

    def score(r, h, c, q, top):
        span = slice(c * ck, (c + 1) * ck)
        s = nn(k_ref[r, span, :], q) + bias_ref[h, span, lanes]
        s_refs[h % 2][span, :] = s
        m = jnp.max(s.reshape(ck // 8, 8, tq), axis=0)
        return m if top is None else jnp.maximum(top, m)

    def mix(r, h, c, top, acc):
        span = slice(c * ck, (c + 1) * ck)
        w = jnp.exp2((s_refs[h % 2][span, :] - top).astype(BF16))
        v = jnp.concatenate(
            [v_ref[r, h * HEAD_DIM : (h + 1) * HEAD_DIM, span], jnp.ones((16, ck), BF16)], axis=0
        )
        o = nn(v, w)
        return o if acc is None else acc + o

    q, top = query(0, 0), None
    for c in range(chunks):
        top = score(0, 0, c, q, top)

    def body(r, top):
        outs = []
        for h in range(HEADS):
            peak = jnp.max(top, axis=0, keepdims=True)
            nh = (h + 1) % HEADS
            nr = r if h < HEADS - 1 else jnp.minimum(r + 1, rows - 1)
            q, top, acc = query(nr, nh), None, None
            for c in range(chunks):
                top = score(nr, nh, c, q, top)
                acc = mix(r, h, c, peak, acc)
            outs.append(acc[:HEAD_DIM] / acc[HEAD_DIM : HEAD_DIM + 1])
        finish(r, lanes, jnp.concatenate(outs, axis=0))
        return top

    lax.fori_loop(0, rows, body, top)


def kernel(
    nx,
    ny,
    tq,
    ck,
    x_ref,
    mask_ref,
    g1_ref,
    w1_ref,
    gb1_ref,
    bw1_ref,
    ow1_ref,
    g2_ref,
    w2_ref,
    gb2_ref,
    bw2_ref,
    ow2_ref,
    g3_ref,
    ti_ref,
    tb_ref,
    to_ref,
    out_ref,
    q_ref,
    k_ref,
    v_ref,
    wt_ref,
    bias_ref,
    kb_ref,
    kc_ref,
    zs_ref,
    st_ref,
    rise_ref,
    sa_ref,
    sb_ref,
    recv_m,
    recv_a,
    recv_b,
    send_z,
    recv_z,
    recv_o,
    ssem,
    rsem,
    fsem,
    lsem,
):
    n = nx * ny
    rows, res, ch = x_ref.shape
    me = lax.axis_index("gx") * ny + lax.axis_index("gy")

    def peer_of(t):
        return lax.rem(me + t, n)

    def coords(p):
        return (p // ny, lax.rem(p, ny))


    def move(kind, src, dst, p, slot):
        return pltpu.make_async_remote_copy(
            src_ref=src,
            dst_ref=dst,
            send_sem=ssem.at[kind, slot],
            recv_sem=rsem.at[kind, slot],
            device_id=coords(p),
            device_id_type=MESH,
        )

    def share(kind, src, dst, p):
        return pltpu.make_async_remote_copy(
            src_ref=src,
            dst_ref=dst,
            send_sem=ssem.at[kind, p],
            recv_sem=rsem.at[kind, me],
            device_id=coords(p),
            device_id_type=MESH,
        )

    gx, gy = lax.axis_index("gx"), lax.axis_index("gy")
    a_ref = out_ref
    core = lax.rem(gx, 2)
    half = nx // 2
    partner = (gx + 1 - 2 * core) * ny + gy

    def line_peer(t):
        return gx * ny + lax.rem(gy + t, ny)

    def plane_peer(t):
        return (lax.rem(gx // 2 + t, half) * 2 + core) * ny + gy

    barrier = pltpu.get_barrier_semaphore()

    def greet(p):
        pl.semaphore_signal(barrier, inc=1, device_id=coords(p), device_id_type=MESH)

    for t in range(1, ny):
        greet(line_peer(t))
    for t in range(1, half):
        greet(plane_peer(t))
    greet(partner)

    def relay(kind, buf, t, s):
        @pl.loop(1, half)
        def _(u):
            q = plane_peer(u)
            pltpu.make_async_remote_copy(
                src_ref=buf.at[s],
                dst_ref=buf.at[s],
                send_sem=fsem.at[kind, t, u],
                recv_sem=rsem.at[kind, s],
                device_id=coords(q),
                device_id_type=MESH,
            ).start()

        hand(kind, buf, s).start()

    def hand(kind, buf, s):
        return move(kind, buf.at[s], buf.at[s], partner, s)

    def gather_start(kind, buf):
        @pl.loop(1, ny)
        def _(t):
            p = line_peer(t)
            pltpu.make_async_remote_copy(
                src_ref=buf.at[me],
                dst_ref=buf.at[me],
                send_sem=lsem.at[kind, t],
                recv_sem=rsem.at[kind, me],
                device_id=coords(p),
                device_id_type=MESH,
            ).start()

        relay(kind, buf, 0, me)

    def gather_finish(kind, buf):
        @pl.loop(1, ny)
        def _(t):
            p = line_peer(t)
            move(kind, buf.at[p], buf.at[p], p, p).wait_recv()
            relay(kind, buf, t, p)

        @pl.loop(0, ny)
        def _(t):
            @pl.loop(1, half)
            def _(u):
                s = plane_peer(u) - gy + lax.rem(gy + t, ny)
                move(kind, buf.at[s], buf.at[s], partner, s).wait_recv()
                hand(kind, buf, s).start()

        @pl.loop(0, ny)
        def _(t):
            @pl.loop(0, half)
            def _(u):
                s = plane_peer(u) - gy + lax.rem(gy + t, ny)
                o = s + (1 - 2 * core) * ny
                move(kind, buf.at[o], buf.at[o], partner, o).wait_recv()
                hand(kind, buf, s).wait_send()

            @pl.loop(1, half)
            def _(u):
                pltpu.make_async_remote_copy(
                    src_ref=buf.at[me],
                    dst_ref=buf.at[me],
                    send_sem=fsem.at[kind, t, u],
                    recv_sem=rsem.at[kind, me],
                    device_id=coords(partner),
                    device_id_type=MESH,
                ).wait_send()

        @pl.loop(1, ny)
        def _(t):
            pltpu.make_async_remote_copy(
                src_ref=buf.at[me],
                dst_ref=buf.at[me],
                send_sem=lsem.at[kind, t],
                recv_sem=rsem.at[kind, me],
                device_id=coords(partner),
                device_id_type=MESH,
            ).wait_send()

    per = tq // rows

    def spread_tile(kind, src, dst, t):
        @pl.loop(0, per)
        def _(u):
            p = t * per + lax.rem(me + u, per)

            @pl.when(p != me)
            def _():
                share(kind, src.at[p], dst.at[me], p).start()

    def spread_finish(kind, src, dst):
        @pl.loop(1, n)
        def _(t):
            p = peer_of(t)
            move(kind, src.at[p], dst.at[p], p, p).wait()

    lane = lax.broadcasted_iota(jnp.int32, (16, 128), 1)
    vec = jnp.zeros((16, 128), F32)
    for t in range(rows):
        vec = jnp.where(lane == lax.rem(me * rows, 128) + t, mask_ref[t].astype(F32), vec)
    recv_m[me] = vec.astype(BF16)

    def norm_row(r, acc):
        normed = layer_norm(x_ref[r].astype(F32), g1_ref[...])
        a_ref[r] = normed
        return acc + bias_rows(bw1_ref[...], r, rows, normed)

    acc = lax.fori_loop(0, rows, norm_row, jnp.zeros((HEADS * rows, res), F32))
    recv_a[me] = acc.astype(BF16)

    pl.semaphore_wait(barrier, ny + half - 1)

    gather_start(2, recv_m)
    gather_start(0, recv_a)

    def turn_weights(w_ref):
        wt_ref[...] = w_ref[...].astype(F32).T.astype(BF16)

    def project(r, normed, w_ref):
        k_ref[r] = nn(normed, w_ref[:, ch : 2 * ch]).astype(BF16)
        q_ref[r] = (nt(wt_ref[:ch], normed) * QSCALE).astype(BF16)
        v_ref[r] = nt(wt_ref[2 * ch : 3 * ch], normed).astype(BF16)

    def gate(r, lanes, o, gb_ref):
        gl = nt(wt_ref[3 * ch :], a_ref[r, lanes, :])
        return (o * jax.nn.sigmoid(gl + gb_ref[...])).T.astype(BF16)

    turn_weights(w1_ref)

    def project_row(r, carry):
        project(r, a_ref[r], w1_ref)
        return carry

    lax.fori_loop(0, rows, project_row, 0)

    gather_finish(2, recv_m)

    kd = 128 // rows
    for t in range(res // 128):
        mask = jnp.sum(recv_m[t * kd : (t + 1) * kd].astype(F32), axis=0)[:1]
        kb = (mask - 1.0) * BIG
        kb_ref[:, t * 128 : (t + 1) * 128] = kb
        kc_ref[t * 128 : (t + 1) * 128, :] = jnp.broadcast_to(kb, (128, 128)).T

    gather_finish(0, recv_a)

    def start_bias(g, carry):
        block = recv_a[pl.ds(g * kd, kd)].astype(F32)
        for h in range(HEADS):
            part = block[:, h * rows : (h + 1) * rows, :].reshape(128, res)
            bias_ref[h, :, pl.ds(pl.multiple_of(g * 128, 128), 128)] = (
                (part + kb_ref[...]) * LOG2E
            ).T
        return carry

    lax.fori_loop(0, res // 128, start_bias, 0)

    def stage(r, z):
        st_ref[:, pl.ds(pl.multiple_of(r * rows, rows), rows), :] = z.reshape(per, rows, ch)

    def start_finish(r, lanes, o):
        z1 = x_ref[r, lanes, :].astype(F32) + nn(gate(r, lanes, o, gb1_ref), ow1_ref[...])
        z1 = z1.astype(BF16).astype(F32)
        stage(r, z1)
        rise_ref[...] = rise_ref[...] + bias_rows(
            bw2_ref[...], r, rows, layer_norm(z1, g2_ref[...])
        )

    def start_tile(t, carry):
        rise_ref[...] = jnp.zeros_like(rise_ref)
        attend_tile(tq, ck, t, q_ref, k_ref, v_ref, bias_ref, (sa_ref, sb_ref), start_finish)
        recv_b[me, :, pl.ds(pl.multiple_of(t * tq, tq), tq)] = rise_ref[...].astype(BF16)
        send_z[pl.ds(t * per, per)] = st_ref[...].astype(BF16)
        spread_tile(3, send_z, recv_z, t)
        return carry

    lax.fori_loop(0, res // tq, start_tile, 0)
    recv_z[me] = send_z[me]
    gather_start(1, recv_b)
    turn_weights(w2_ref)
    spread_finish(3, send_z, recv_z)

    def end_project(d, carry):
        z1 = zs_ref[:, pl.ds(d, rows, stride=rows), :].reshape(res, ch)
        normed = layer_norm(z1, g2_ref[...])
        a_ref[d] = normed
        project(d, normed, w2_ref)
        return carry

    zs_ref[...] = recv_z[...].astype(F32)
    lax.fori_loop(0, rows, end_project, 0)
    gather_finish(1, recv_b)

    def end_bias(g, carry):
        block = recv_b[pl.ds(g * kd, kd)].astype(F32)
        keys = pl.ds(pl.multiple_of(g * 128, 128), 128)
        kc = kc_ref[keys, :]
        for h in range(HEADS):
            part = block[:, h * rows : (h + 1) * rows, :].reshape(128, res)
            for t in range(res // 128):
                span = slice(t * 128, (t + 1) * 128)
                bias_ref[h, keys, span] = (part[:, span] + kc) * LOG2E
        return carry

    lax.fori_loop(0, res // 128, end_bias, 0)

    def end_tile(t, carry):
        def end_finish(r, lanes, o):
            z1 = zs_ref[pl.ds(t * per, per), pl.ds(r, rows, stride=rows), :].reshape(tq, ch)
            z2 = z1 + nn(gate(r, lanes, o, gb2_ref), ow2_ref[...])
            z2 = z2.astype(BF16).astype(F32)
            hid = nn(layer_norm(z2, g3_ref[...]), ti_ref[...]) + tb_ref[...]
            hid = jnp.maximum(hid, 0.0).astype(BF16)
            stage(r, z2 + nn(hid, to_ref[...]))

        attend_tile(tq, ck, t, q_ref, k_ref, v_ref, bias_ref, (sa_ref, sb_ref), end_finish)
        send_z[pl.ds(t * per, per)] = st_ref[...].astype(BF16)
        spread_tile(4, send_z, recv_o, t)
        return carry

    lax.fori_loop(0, res // tq, end_tile, 0)
    recv_o[me] = send_z[me]
    spread_finish(4, send_z, recv_o)

    zs_ref[...] = recv_o[...].astype(F32)

    def out_row(r, carry):
        out_ref[r] = zs_ref[:, pl.ds(r, rows, stride=rows), :].reshape(res, ch).astype(BF16)
        return carry

    lax.fori_loop(0, rows, out_row, 0)


def solution(mesh):
    nx, ny = mesh.shape["gx"], mesh.shape["gy"]
    n = nx * ny

    def local(x, mask, g1, w1, gb1, bw1, ow1, g2, w2, gb2, bw2, ow2, g3, ti, tb, to):
        rows, res, ch = x.shape
        tq, ck = min(res, 256), min(res, 256)
        vmem = pl.BlockSpec(memory_space=pltpu.VMEM)
        row = lambda t: t.reshape(1, -1)
        return pl.pallas_call(
            functools.partial(kernel, nx, ny, tq, ck),
            out_shape=jax.ShapeDtypeStruct(x.shape, x.dtype),
            in_specs=[vmem, pl.BlockSpec(memory_space=pltpu.SMEM)] + [vmem] * 14,
            out_specs=vmem,
            scratch_shapes=[
                pltpu.VMEM((rows, ch, res), BF16),
                pltpu.VMEM((rows, res, ch), BF16),
                pltpu.VMEM((rows, ch, res), BF16),
                pltpu.VMEM((4 * ch, ch), BF16),
                pltpu.VMEM((HEADS, res, res), F32),
                pltpu.VMEM((1, res), F32),
                pltpu.VMEM((res, 128), F32),
                pltpu.VMEM((n, rows * rows, ch), F32),
                pltpu.VMEM((tq // rows, rows * rows, ch), F32),
                pltpu.VMEM((HEADS * rows, tq), F32),
                pltpu.VMEM((res, tq), F32),
                pltpu.VMEM((res, tq), F32),
                pltpu.VMEM((n, 16, 128), BF16),
                pltpu.VMEM((n, HEADS * rows, res), BF16),
                pltpu.VMEM((n, HEADS * rows, res), BF16),
                pltpu.VMEM((n, rows * rows, ch), BF16),
                pltpu.VMEM((n, rows * rows, ch), BF16),
                pltpu.VMEM((n, rows * rows, ch), BF16),
                pltpu.SemaphoreType.DMA((5, n)),
                pltpu.SemaphoreType.DMA((5, n)),
                pltpu.SemaphoreType.DMA((3, ny, nx // 2)),
                pltpu.SemaphoreType.DMA((3, ny)),
            ],
            compiler_params=pltpu.CompilerParams(
                collective_id=0, has_side_effects=True, vmem_limit_bytes=66 * 1000 * 1000
            ),
        )(
            x, mask, row(g1), w1, gb1.reshape(-1, 1), bw1.T, ow1, row(g2), w2,
            gb2.reshape(-1, 1), bw2.T, ow2,
            row(g3), ti, row(tb), to,
        )

    placed = (P(("gx", "gy"), None, None), P(("gx", "gy"))) + (P(),) * 14
    return jax.shard_map(
        local, mesh=mesh, in_specs=placed, out_specs=P(("gx", "gy"), None, None), check_vma=False
    )
```

profile of v0, /device:TPU:1, one launch (start us, length us, event | category | flops | bytes accessed | tf_op | source)
XLA Modules:
  0.0 327.8 jit_solution(10603796457354785784)
XLA Ops:
  0.0 1.4 copy.17.gb1_ref
  1.4 1.4 copy.18.gb2_ref
  2.8 322.0 %shard_map.154 = bf16[8,1024,128]{2,1,0:T(8,128)(2,1)} custom-call(bf16[8,1024,128]{2,1,0:T(8,128)(2,1)} %x_ref.1, s32[8]{0:T(128)} %mask_ref.1, f32[1,128]{1,0:T(1,128)} %bitcast.13, bf16[128,512]{1,0:T(8,128)(2,1)} %w1_ref.1, f32[128,1]{1,0:T(8,128)} %copy.17.gb1_ref, bf16[4,128]{1,0:T(4,128)(2,1)} %bitcast.9, bf16[128,128]{1,0:T(8,128)(2,1)} %ow1_ref.1, ...), custom_call_target="tpu_custom_call" | custom-call | tf_op jit(solution)/shard_map/pallas_call | solution.py:433
  324.7 3.1 copy.20
where the time goes:
time: 334 us; the launch traced here: 328 us
  Pallas kernels  322 us (96%)
  local copies, waits for them, and re-layouts  5.83 us (2%)
    pallas_call x1, Pallas kernels, local(): pl.pallas_call(functools.partial(kernel, nx, ny, tq, ck), out_shape=jax.S...  322 us

commit v1 on v0

v1 whole, which is shorter than its diff:
```python
import functools
import math

import jax
import jax.numpy as jnp
from jax import lax
from jax.experimental import pallas as pl
from jax.experimental.pallas import tpu as pltpu
from jax.sharding import PartitionSpec as P

HEADS = 4
HEAD_DIM = 32
BIG = 1000000000.0
LOG2E = math.log2(math.e)
QSCALE = HEAD_DIM ** (-0.5) * LOG2E
MESH = pl.DeviceIdType.MESH
F32 = jnp.float32
BF16 = jnp.bfloat16


def nn(a, b):
    return lax.dot_general(a, b, (((1,), (0,)), ((), ())), preferred_element_type=F32)


def nt(a, b):
    return lax.dot_general(a, b, (((1,), (1,)), ((), ())), preferred_element_type=F32)


def layer_norm(x, gain):
    mean = jnp.mean(x, axis=-1, keepdims=True)
    cent = x - mean
    var = jnp.mean(cent * cent, axis=-1, keepdims=True)
    return (cent * lax.rsqrt(var + 1e-05) * gain).astype(BF16)


def bias_rows(w, r, rows, normed):
    shape = (HEADS * rows, HEADS)
    place = lax.broadcasted_iota(jnp.int32, shape, 0) == (
        lax.broadcasted_iota(jnp.int32, shape, 1) * rows + r
    )
    spread = nn(place.astype(F32).astype(BF16), w).astype(BF16)
    return nt(spread, normed)


def attend_tile(ck, t, q_ref, k_ref, v_ref, bias_ref, s_refs, finish):
    rows, res, ch = k_ref.shape
    tq = s_refs[0].shape[1]
    lanes = pl.ds(pl.multiple_of(t * tq, tq), tq)
    chunks = res // ck

    def query(r, h):
        q = q_ref[r, :, lanes]
        row = lax.broadcasted_iota(jnp.int32, q.shape, 0)
        return jnp.where((row >= h * HEAD_DIM) & (row < (h + 1) * HEAD_DIM), q, jnp.zeros_like(q))

    def score(r, h, c, q, top):
        span = slice(c * ck, (c + 1) * ck)
        s = nn(k_ref[r, span, :], q) + bias_ref[h, span, lanes]
        s_refs[h % 2][span, :] = s
        m = jnp.max(s.reshape(ck // 8, 8, tq), axis=0)
        return m if top is None else jnp.maximum(top, m)

    def mix(r, h, c, top, acc):
        span = slice(c * ck, (c + 1) * ck)
        w = jnp.exp2((s_refs[h % 2][span, :] - top).astype(BF16))
        v = jnp.concatenate(
            [v_ref[r, h * HEAD_DIM : (h + 1) * HEAD_DIM, span], jnp.ones((16, ck), BF16)], axis=0
        )
        o = nn(v, w)
        return o if acc is None else acc + o

    q, top = query(0, 0), None
    for c in range(chunks):
        top = score(0, 0, c, q, top)

    def body(r, top):
        outs = []
        for h in range(HEADS):
            peak = jnp.max(top, axis=0, keepdims=True)
            nh = (h + 1) % HEADS
            nr = r if h < HEADS - 1 else jnp.minimum(r + 1, rows - 1)
            q, top, acc = query(nr, nh), None, None
            for c in range(chunks):
                top = score(nr, nh, c, q, top)
                acc = mix(r, h, c, peak, acc)
            outs.append(acc[:HEAD_DIM] / acc[HEAD_DIM : HEAD_DIM + 1])
        finish(r, jnp.concatenate(outs, axis=0))
        return top

    lax.fori_loop(0, rows, body, top)


class Gather:
    def __init__(self, place, ssem, rsem):
        self.place, self.ssem, self.rsem = place, ssem, rsem

    def copy(self, inst, kind, src, dst, to):
        return pltpu.make_async_remote_copy(
            src_ref=src,
            dst_ref=dst,
            send_sem=self.ssem.at[inst, kind],
            recv_sem=self.rsem.at[inst, kind],
            device_id=self.place(*to),
            device_id_type=MESH,
        )

    def setup(self, me, sizes):
        self.x, self.core, self.plane = me
        self.xs, self.planes = sizes
        self.other = 1 - self.core

    def at(self, step):
        return lax.rem(self.x + step, self.xs)

    def fan(self, inst, kind, slot):
        @pl.loop(1, self.planes)
        def _(u):
            p = lax.rem(self.plane + u, self.planes)
            self.copy(inst, kind, slot, slot, (self.x, self.core, p)).start()

    def fanned(self, inst, kind, buf):
        rest = buf.at[self.x, self.core, pl.ds(0, self.planes - 1)]
        return self.copy(inst, kind, rest, rest, (self.x, self.other, self.plane))

    def line(self, inst, kind, buf, step):
        part = buf.at[self.x, self.core]
        return self.copy(inst, kind, part, part, (self.at(step), self.core, self.plane))

    def hand(self, inst, kind, buf, step, core=None):
        part = buf.at[self.at(step), self.core if core is None else core]
        return self.copy(inst, kind, part, part, (self.x, self.other, self.plane))

    def far(self, inst, slot):
        half = self.xs // 2
        return self.copy(inst, 1, slot, slot, (self.at(half), self.core, self.plane))

    def first(self, inst, buf):
        slot = buf.at[self.x, self.core, self.plane]
        self.far(inst, slot).start()
        self.fan(inst, 0, slot)

    def second(self, inst, buf, buf_far):
        slot = buf_far.at[self.at(self.xs // 2), self.core, self.plane]
        self.far(inst, slot).wait_recv()
        self.fan(inst, 2, slot)
        self.fanned(inst, 0, buf).wait_recv()
        self.hand(inst, 5, buf, 0).start()
        self.line(inst, 3, buf, 1).start()
        self.line(inst, 4, buf, self.xs - 1).start()

    def third_far(self, inst, buf_far):
        self.fanned(inst, 2, buf_far).wait_recv()
        self.hand(inst, 6, buf_far, self.xs // 2).start()

    def third_near(self, inst, buf_up, buf_down):
        self.line(inst, 4, buf_up, 1).wait_recv()
        self.hand(inst, 7, buf_up, 1).start()
        self.line(inst, 3, buf_down, 1).wait_recv()
        self.hand(inst, 8, buf_down, self.xs - 1).start()

    def handed(self, inst, kind, buf, step):
        self.hand(inst, kind, buf, step, self.other).wait_recv()

    def drain(self, inst, buf):
        slot = buf.at[self.x, self.core, self.plane]
        self.far(inst, slot).wait_send()
        self.fanned(inst, 0, buf).wait_send()
        self.fanned(inst, 2, buf).wait_send()
        self.line(inst, 3, buf, 1).wait_send()
        self.line(inst, 4, buf, 1).wait_send()
        for kind in (5, 6, 7, 8):
            self.hand(inst, kind, buf, 0).wait_send()


def kernel(
    nx,
    ny,
    ck,
    x_ref,
    mask_ref,
    g1_ref,
    w1_ref,
    gb1_ref,
    bw1_ref,
    ow1_ref,
    g2_ref,
    w2_ref,
    gb2_ref,
    bw2_ref,
    ow2_ref,
    g3_ref,
    ti_ref,
    tb_ref,
    to_ref,
    out_ref,
    q_ref,
    k_ref,
    v_ref,
    wt_ref,
    bias_ref,
    kb_ref,
    kc_ref,
    zs_ref,
    st_ref,
    rise_ref,
    sa_ref,
    sb_ref,
    recv_m,
    recv_a,
    recv_b,
    send_z,
    recv_z,
    recv_o,
    ssem,
    rsem,
    zsem,
):
    n = nx * ny
    xs, planes = nx // 4, 2 * ny
    rows, res, ch = x_ref.shape
    tq = res // xs
    a_ref = out_ref
    gx, gy = lax.axis_index("gx"), lax.axis_index("gy")
    me = gx * ny + gy
    core = lax.rem(gx, 2)
    x = lax.rem(gx // 2, xs)
    low = gx // (2 * xs)
    plane = low * ny + gy
    run = 2 * ny

    def place(x, core, plane):
        return (plane // ny * (2 * xs) + x * 2 + core, lax.rem(plane, ny))

    g = Gather(place, ssem, rsem)
    g.setup((x, core, plane), (xs, planes))
    barrier = pltpu.get_barrier_semaphore()

    def greet(*to):
        pl.semaphore_signal(barrier, inc=1, device_id=place(*to), device_id_type=MESH)

    for u in range(1, planes):
        greet(x, core, lax.rem(plane + u, planes))
    for u in range(1, xs):
        greet(g.at(u), core, plane)
    greet(x, 1 - core, plane)

    lane = lax.broadcasted_iota(jnp.int32, (16, 128), 1)
    vec = jnp.zeros((16, 128), F32)
    for t in range(rows):
        vec = jnp.where(lane == lax.rem(me * rows, 128) + t, mask_ref[t].astype(F32), vec)
    recv_m[x, core, plane] = vec.astype(BF16)

    pl.semaphore_wait(barrier, planes - 1 + xs - 1 + 1)
    g.first(0, recv_m)

    def norm_row(r, acc):
        normed = layer_norm(x_ref[r].astype(F32), g1_ref[...])
        a_ref[r] = normed
        return acc + bias_rows(bw1_ref[...], r, rows, normed)

    with jax.named_scope("norm"):
        acc = lax.fori_loop(0, rows, norm_row, jnp.zeros((HEADS * rows, res), F32))
        recv_a[x, core, plane] = acc.astype(BF16)

    g.first(1, recv_a)
    with jax.named_scope("mask2"):
        g.second(0, recv_m, recv_m)

    def turn_weights(w_ref):
        wt_ref[...] = w_ref[...].astype(F32).T.astype(BF16)

    def project(r, normed, w_ref):
        k_ref[r] = nn(normed, w_ref[:, ch : 2 * ch]).astype(BF16)
        q = (nt(wt_ref[:ch], normed) * QSCALE).astype(BF16)
        for b in range(2 * xs):
            to = (b % xs * 2 + b // xs) * 128
            q_ref[r, :, to : to + 128] = q[:, b * 128 : (b + 1) * 128]
        v_ref[r] = nt(wt_ref[2 * ch : 3 * ch], normed).astype(BF16)

    def both(t, size):
        return [pl.ds(pl.multiple_of((t + e * xs) * size, size), size) for e in range(2)]

    def gate(r, t, o, gb_ref):
        a = jnp.concatenate([a_ref[r, span, :] for span in both(t, 128)], axis=0)
        gl = nt(wt_ref[3 * ch :], a)
        return (o * jax.nn.sigmoid(gl + gb_ref[...])).T.astype(BF16)

    turn_weights(w1_ref)

    def project_row(r, carry):
        project(r, a_ref[r], w1_ref)
        return carry

    with jax.named_scope("project"):
        lax.fori_loop(0, rows, project_row, 0)
    with jax.named_scope("mask3"):
        g.third_far(0, recv_m)
        g.third_near(0, recv_m, recv_m)
    with jax.named_scope("a2"):
        g.second(1, recv_a, recv_a)
    with jax.named_scope("mask4"):
        g.handed(0, 5, recv_m, 0)
        g.handed(0, 6, recv_m, xs // 2)
        g.handed(0, 7, recv_m, 1)
        g.handed(0, 8, recv_m, xs - 1)

    for b in range(2 * xs):
        part = recv_m[b % xs, :, b // xs * ny : (b // xs + 1) * ny].astype(F32)
        mask = jnp.sum(jnp.sum(part, axis=0), axis=0)[:1]
        kb = (mask - 1.0) * BIG
        kb_ref[:, b * 128 : (b + 1) * 128] = kb
        kc_ref[b * 128 : (b + 1) * 128, :] = jnp.broadcast_to(kb, (128, 128)).T

    def start_bias(t):
        for e in range(2):
            blocks = [
                recv_a[t, c, e * ny : (e + 1) * ny].astype(F32) for c in range(2)
            ]
            for h in range(HEADS):
                part = jnp.concatenate(
                    [b[:, h * rows : (h + 1) * rows, :].reshape(64, res) for b in blocks], axis=0
                )
                to = pl.ds(pl.multiple_of(t * tq + e * 128, 128), 128)
                bias_ref[h, :, to] = ((part + kb_ref[...]) * LOG2E).T

    def stage(r, z):
        st_ref[:, pl.ds(pl.multiple_of(r * rows, rows), rows), :] = z.reshape(
            tq // rows, rows, ch
        )

    def ship(kind, dst, t):
        for e, span in enumerate(both(t, run)):
            send_z[span] = st_ref[e * run : (e + 1) * run].astype(BF16)

        @pl.loop(0, 2 * run)
        def _(u):
            v = lax.rem(u + plane * 2 + core, 2 * run)
            c, p = lax.rem(v, 2), v // 2
            to = place(t, c, p)
            d = to[0] * ny + to[1]

            @pl.when(d != me)
            def _():
                pltpu.make_async_remote_copy(
                    src_ref=send_z.at[d],
                    dst_ref=dst.at[me],
                    send_sem=zsem.at[kind, 0],
                    recv_sem=zsem.at[kind, 1],
                    device_id=to,
                    device_id_type=MESH,
                ).start()

    def shipped(kind, dst):
        dst[me] = send_z[me]
        rest = pl.ds(0, n - 1)
        pltpu.make_async_remote_copy(
            src_ref=send_z.at[rest],
            dst_ref=dst.at[rest],
            send_sem=zsem.at[kind, 0],
            recv_sem=zsem.at[kind, 1],
            device_id=place(x, 1 - core, plane),
            device_id_type=MESH,
        ).wait()

    def tile_of(s, step=0):
        away = jnp.where(s == 0, 0, jnp.where(s == 1, xs // 2, jnp.where(s == 2, 1, xs - 1)))
        return lax.rem(x + step + away, xs)

    def rise_second(s):
        t = tile_of(s)
        g.second(2 + s, recv_b.at[t], recv_b.at[tile_of(s, xs // 2)])

    def rise_third(s):
        g.third_far(2 + s, recv_b.at[tile_of(s, xs // 2)])
        g.third_near(2 + s, recv_b.at[tile_of(s, 1)], recv_b.at[tile_of(s, xs - 1)])

    def start_tile(s, carry):
        t = tile_of(s)

        @pl.when(s == 0)
        def _():
            with jax.named_scope("wait0"):
                g.handed(1, 5, recv_a, 0)

        @pl.when(s == 1)
        def _():
            with jax.named_scope("wait1"):
                g.third_far(1, recv_a)
                g.handed(1, 6, recv_a, xs // 2)

        @pl.when(s == 2)
        def _():
            with jax.named_scope("wait2"):
                g.third_near(1, recv_a, recv_a)
                g.handed(1, 7, recv_a, 1)

        @pl.when(s == 3)
        def _():
            with jax.named_scope("wait3"):
                g.handed(1, 8, recv_a, xs - 1)

        with jax.named_scope("biasa"):
            start_bias(t)
        rise_ref[...] = jnp.zeros_like(rise_ref)

        def start_finish(r, o):
            old = jnp.concatenate([x_ref[r, span, :] for span in both(t, 128)], axis=0)
            z1 = old.astype(F32) + nn(gate(r, t, o, gb1_ref), ow1_ref[...])
            z1 = z1.astype(BF16).astype(F32)
            stage(r, z1)
            rise_ref[...] = rise_ref[...] + bias_rows(
                bw2_ref[...], r, rows, layer_norm(z1, g2_ref[...])
            )

            @pl.when((s > 0) & (r == rows // 2 - 1))
            def _():
                with jax.named_scope("rise2"):
                    rise_second(s - 1)

            @pl.when((s > 0) & (r == rows - 1))
            def _():
                with jax.named_scope("rise3"):
                    rise_third(s - 1)

        with jax.named_scope("att1"):
            attend_tile(ck, t, q_ref, k_ref, v_ref, bias_ref, (sa_ref, sb_ref), start_finish)
        recv_b[t, x, core, plane] = rise_ref[...].astype(BF16)
        with jax.named_scope("ship1"):
            g.first(2 + s, recv_b.at[t])
            ship(0, recv_z, t)
        return carry

    lax.fori_loop(0, xs, start_tile, 0)
    turn_weights(w2_ref)
    with jax.named_scope("rise2e"):
        rise_second(xs - 1)
    with jax.named_scope("waitz"):
        shipped(0, recv_z)
    zs_ref[...] = recv_z[...].astype(F32)

    def end_project(d, carry):
        z1 = zs_ref[:, pl.ds(d, rows, stride=rows), :].reshape(res, ch)
        normed = layer_norm(z1, g2_ref[...])
        a_ref[d] = normed
        project(d, normed, w2_ref)
        return carry

    with jax.named_scope("rise3e"):
        rise_third(xs - 1)
    with jax.named_scope("project2"):
        lax.fori_loop(0, rows, end_project, 0)

    def rise_done(s, carry):
        g.handed(2 + s, 5, recv_b.at[tile_of(s)], 0)
        g.handed(2 + s, 6, recv_b.at[tile_of(s, xs // 2)], xs // 2)
        g.handed(2 + s, 7, recv_b.at[tile_of(s, 1)], 1)
        g.handed(2 + s, 8, recv_b.at[tile_of(s, xs - 1)], xs - 1)
        return carry

    with jax.named_scope("handed"):
        lax.fori_loop(0, xs, rise_done, 0)

    def end_bias(t):
        def keys_of(b, carry):
            e, c = lax.rem(b // 2, 2), lax.rem(b, 2)
            keys = pl.ds(pl.multiple_of((e * 2 * xs + b // 4 * 2 + c) * 64, 64), 64)
            kc = kc_ref[keys, :]
            block = recv_b[t, b // 4, c, pl.ds(e * ny, ny)].astype(F32)
            for h in range(HEADS):
                part = block[:, h * rows : (h + 1) * rows, :].reshape(64, tq)
                for w in range(tq // 128):
                    to = pl.ds(pl.multiple_of(t * tq + w * 128, 128), 128)
                    bias_ref[h, keys, to] = (part[:, w * 128 : (w + 1) * 128] + kc) * LOG2E
            return carry

        lax.fori_loop(0, 4 * xs, keys_of, 0)

    def end_tile(s, carry):
        t = tile_of(s)
        with jax.named_scope("biasb"):
            end_bias(t)

        def end_finish(r, o):
            z1 = jnp.concatenate(
                [
                    zs_ref[span, pl.ds(r, rows, stride=rows), :].reshape(128, ch)
                    for span in both(t, run)
                ],
                axis=0,
            )
            z2 = z1 + nn(gate(r, t, o, gb2_ref), ow2_ref[...])
            z2 = z2.astype(BF16).astype(F32)
            hid = nn(layer_norm(z2, g3_ref[...]), ti_ref[...]) + tb_ref[...]
            hid = jnp.maximum(hid, 0.0).astype(BF16)
            stage(r, z2 + nn(hid, to_ref[...]))

        with jax.named_scope("att2"):
            attend_tile(ck, t, q_ref, k_ref, v_ref, bias_ref, (sa_ref, sb_ref), end_finish)
        with jax.named_scope("ship2"):
            ship(1, recv_o, t)
        return carry

    lax.fori_loop(0, xs, end_tile, 0)
    with jax.named_scope("drain"):
        g.drain(0, recv_m)
        g.drain(1, recv_a)

        def drain_rise(s, carry):
            g.drain(2 + s, recv_b.at[tile_of(s)])
            return carry

        lax.fori_loop(0, xs, drain_rise, 0)
    with jax.named_scope("waito"):
        shipped(1, recv_o)

    zs_ref[...] = recv_o[...].astype(F32)

    def out_row(r, carry):
        out_ref[r] = zs_ref[:, pl.ds(r, rows, stride=rows), :].reshape(res, ch).astype(BF16)
        return carry

    with jax.named_scope("outrow"):
        lax.fori_loop(0, rows, out_row, 0)


def solution(mesh):
    nx, ny = mesh.shape["gx"], mesh.shape["gy"]
    n, xs = nx * ny, nx // 4

    def local(x, mask, g1, w1, gb1, bw1, ow1, g2, w2, gb2, bw2, ow2, g3, ti, tb, to):
        rows, res, ch = x.shape
        tq, ck = res // xs, 256
        vmem = pl.BlockSpec(memory_space=pltpu.VMEM)
        row = lambda t: t.reshape(1, -1)
        return pl.pallas_call(
            functools.partial(kernel, nx, ny, ck),
            out_shape=jax.ShapeDtypeStruct(x.shape, x.dtype),
            in_specs=[vmem, pl.BlockSpec(memory_space=pltpu.SMEM)] + [vmem] * 14,
            out_specs=vmem,
            scratch_shapes=[
                pltpu.VMEM((rows, ch, res), BF16),
                pltpu.VMEM((rows, res, ch), BF16),
                pltpu.VMEM((rows, ch, res), BF16),
                pltpu.VMEM((4 * ch, ch), BF16),
                pltpu.VMEM((HEADS, res, res), F32),
                pltpu.VMEM((1, res), F32),
                pltpu.VMEM((res, 128), F32),
                pltpu.VMEM((n, rows * rows, ch), F32),
                pltpu.VMEM((tq // rows, rows * rows, ch), F32),
                pltpu.VMEM((HEADS * rows, tq), F32),
                pltpu.VMEM((res, tq), F32),
                pltpu.VMEM((res, tq), F32),
                pltpu.VMEM((xs, 2, 2 * ny, 16, 128), BF16),
                pltpu.VMEM((xs, 2, 2 * ny, HEADS * rows, res), BF16),
                pltpu.VMEM((xs, xs, 2, 2 * ny, HEADS * rows, tq), BF16),
                pltpu.VMEM((n, rows * rows, ch), BF16),
                pltpu.VMEM((n, rows * rows, ch), BF16),
                pltpu.VMEM((n, rows * rows, ch), BF16),
                pltpu.SemaphoreType.DMA((2 + xs, 9)),
                pltpu.SemaphoreType.DMA((2 + xs, 9)),
                pltpu.SemaphoreType.DMA((2, 2)),
            ],
            compiler_params=pltpu.CompilerParams(
                collective_id=0, has_side_effects=True, vmem_limit_bytes=66 * 1000 * 1000
            ),
        )(
            x, mask, row(g1), w1, gb1.reshape(-1, 1), bw1.T, ow1, row(g2), w2,
            gb2.reshape(-1, 1), bw2.T, ow2, row(g3), ti, row(tb), to,
        )

    placed = (P(("gx", "gy"), None, None), P(("gx", "gy"))) + (P(),) * 14
    return jax.shard_map(
        local, mesh=mesh, in_specs=placed, out_specs=P(("gx", "gy"), None, None), check_vma=False
    )
```

time: 334 us -> 248 us (0.74); the launches traced: 328 us -> 248 us
  Pallas kernels: 322 us -> 242 us
    pallas_call x1, Pallas kernels: 322 us -> 242 us  [local(): pl.pallas_call(functools.partial(kernel, nx, ny, ck), out_shape=jax.Shape...]
where the time goes in v1:
time: 248 us
  Pallas kernels  242 us (98%)
  local copies, waits for them, and re-layouts  5.83 us (2%)
    pallas_call x1, Pallas kernels, local(): pl.pallas_call(functools.partial(kernel, nx, ny, ck), out_shape=jax.Shape...  242 us

profile of v1, /device:TPU:1, one launch (start us, length us, event | category | flops | bytes accessed | tf_op | source)
XLA Modules:
  0.0 247.6 jit_solution(6108039407186783476)
XLA Ops:
  0.0 1.4 copy.17.gb1_ref
  1.4 1.4 copy.18.gb2_ref
  2.8 241.8 %shard_map.154 = bf16[8,1024,128]{2,1,0:T(8,128)(2,1)} custom-call(bf16[8,1024,128]{2,1,0:T(8,128)(2,1)} %x_ref.1, s32[8]{0:T(128)} %mask_ref.1, f32[1,128]{1,0:T(1,128)} %bitcast.13, bf16[128,512]{1,0:T(8,128)(2,1)} %w1_ref.1, f32[128,1]{1,0:T(8,128)} %copy.17.gb1_ref, bf16[4,128]{1,0:T(4,128)(2,1)} %bitcast.9, bf16[128,128]{1,0:T(8,128)(2,1)} %ow1_ref.1, ...), custom_call_target="tpu_custom_call" | custom-call | tf_op jit(solution)/shard_map/pallas_call | solution.py:535
  244.6 3.1 %copy.20 = bf16[8,1024,128]{2,1,0:T(8,128)(2,1)} copy(bf16[8,1024,128]{2,1,0:T(8,128)(2,1)} %shard_map.154) | data formatting | bytes 4194304

commit v2 on v1

--- a/solution.py
+++ b/solution.py
@@ -42,7 +42,7 @@
     return nt(spread, normed)
 
 
-def attend_tile(ck, t, q_ref, k_ref, v_ref, bias_ref, s_refs, finish):
+def attend_tile(ck, t, q_ref, k_ref, v_ref, bias_ref, s_refs, o_ref, after):
     rows, res, ch = k_ref.shape
     tq = s_refs[0].shape[1]
     lanes = pl.ds(pl.multiple_of(t * tq, tq), tq)
@@ -84,7 +84,8 @@
                 top = score(nr, nh, c, q, top)
                 acc = mix(r, h, c, peak, acc)
             outs.append(acc[:HEAD_DIM] / acc[HEAD_DIM : HEAD_DIM + 1])
-        finish(r, jnp.concatenate(outs, axis=0))
+        o_ref[r] = jnp.concatenate(outs, axis=0)
+        after(r)
         return top
 
     lax.fori_loop(0, rows, body, top)
@@ -205,6 +206,7 @@
     rise_ref,
     sa_ref,
     sb_ref,
+    o_ref,
     recv_m,
     recv_a,
     recv_b,
@@ -280,10 +282,19 @@
     def both(t, size):
         return [pl.ds(pl.multiple_of((t + e * xs) * size, size), size) for e in range(2)]
 
-    def gate(r, t, o, gb_ref):
-        a = jnp.concatenate([a_ref[r, span, :] for span in both(t, 128)], axis=0)
-        gl = nt(wt_ref[3 * ch :], a)
-        return (o * jax.nn.sigmoid(gl + gb_ref[...])).T.astype(BF16)
+    def mixed(batch, t, gb_ref, ow_ref):
+        a = [jnp.concatenate([a_ref[r, span, :] for span in both(t, 128)], axis=0) for r in batch]
+        gl = [nt(wt_ref[3 * ch :], v) for v in a]
+        gated = [o_ref[r] * jax.nn.sigmoid(v + gb_ref[...]) for r, v in zip(batch, gl)]
+        gated = [v.T.astype(BF16) for v in gated]
+        return [nn(v, ow_ref[...]) for v in gated]
+
+    def batches(fn):
+        def run(i, carry):
+            fn([i * 8 + e for e in range(8)])
+            return carry
+
+        lax.fori_loop(0, rows // 8, run, 0)
 
     turn_weights(w1_ref)
 
@@ -401,17 +412,17 @@
 
         with jax.named_scope("biasa"):
             start_bias(t)
-        rise_ref[...] = jnp.zeros_like(rise_ref)
-
-        def start_finish(r, o):
-            old = jnp.concatenate([x_ref[r, span, :] for span in both(t, 128)], axis=0)
-            z1 = old.astype(F32) + nn(gate(r, t, o, gb1_ref), ow1_ref[...])
-            z1 = z1.astype(BF16).astype(F32)
-            stage(r, z1)
-            rise_ref[...] = rise_ref[...] + bias_rows(
-                bw2_ref[...], r, rows, layer_norm(z1, g2_ref[...])
-            )
-
+        def start_finish(batch):
+            out = mixed(batch, t, gb1_ref, ow1_ref)
+            old = [jnp.concatenate([x_ref[r, p, :] for p in both(t, 128)], axis=0) for r in batch]
+            z1 = [(u.astype(F32) + v).astype(BF16).astype(F32) for u, v in zip(old, out)]
+            for r, v in zip(batch, z1):
+                stage(r, v)
+            normed = [layer_norm(v, g2_ref[...]) for v in z1]
+            part = [bias_rows(bw2_ref[...], r, rows, v) for r, v in zip(batch, normed)]
+            rise_ref[...] = rise_ref[...] + sum(part[1:], part[0])
+
+        def start_after(r):
             @pl.when((s > 0) & (r == rows // 2 - 1))
             def _():
                 with jax.named_scope("rise2"):
@@ -423,7 +434,11 @@
                     rise_third(s - 1)
 
         with jax.named_scope("att1"):
-            attend_tile(ck, t, q_ref, k_ref, v_ref, bias_ref, (sa_ref, sb_ref), start_finish)
+            attend_tile(ck, t, q_ref, k_ref, v_ref, bias_ref, (sa_ref, sb_ref), o_ref,
+                start_after)
+        with jax.named_scope("tail1"):
+            rise_ref[...] = jnp.zeros_like(rise_ref)
+            batches(start_finish)
         recv_b[t, x, core, plane] = rise_ref[...].astype(BF16)
         with jax.named_scope("ship1"):
             g.first(2 + s, recv_b.at[t])
@@ -480,22 +495,31 @@
         with jax.named_scope("biasb"):
             end_bias(t)
 
-        def end_finish(r, o):
-            z1 = jnp.concatenate(
-                [
-                    zs_ref[span, pl.ds(r, rows, stride=rows), :].reshape(128, ch)
-                    for span in both(t, run)
-                ],
-                axis=0,
-            )
-            z2 = z1 + nn(gate(r, t, o, gb2_ref), ow2_ref[...])
-            z2 = z2.astype(BF16).astype(F32)
-            hid = nn(layer_norm(z2, g3_ref[...]), ti_ref[...]) + tb_ref[...]
-            hid = jnp.maximum(hid, 0.0).astype(BF16)
-            stage(r, z2 + nn(hid, to_ref[...]))
+        def end_finish(batch):
+            out = mixed(batch, t, gb2_ref, ow2_ref)
+            z1 = [
+                jnp.concatenate(
+                    [
+                        zs_ref[span, pl.ds(r, rows, stride=rows), :].reshape(128, ch)
+                        for span in both(t, run)
+                    ],
+                    axis=0,
+                )
+                for r in batch
+            ]
+            z2 = [(u + v).astype(BF16).astype(F32) for u, v in zip(z1, out)]
+            normed = [layer_norm(v, g3_ref[...]) for v in z2]
+            hid = [nn(v, ti_ref[...]) + tb_ref[...] for v in normed]
+            hid = [jnp.maximum(v, 0.0).astype(BF16) for v in hid]
+            last = [nn(v, to_ref[...]) for v in hid]
+            for r, u, v in zip(batch, z2, last):
+                stage(r, u + v)
 
         with jax.named_scope("att2"):
-            attend_tile(ck, t, q_ref, k_ref, v_ref, bias_ref, (sa_ref, sb_ref), end_finish)
+            attend_tile(ck, t, q_ref, k_ref, v_ref, bias_ref, (sa_ref, sb_ref), o_ref,
+                lambda r: None)
+        with jax.named_scope("tail2"):
+            batches(end_finish)
         with jax.named_scope("ship2"):
             ship(1, recv_o, t)
         return carry
@@ -529,7 +553,7 @@
 
     def local(x, mask, g1, w1, gb1, bw1, ow1, g2, w2, gb2, bw2, ow2, g3, ti, tb, to):
         rows, res, ch = x.shape
-        tq, ck = res // xs, 256
+        tq, ck = res // xs, 512
         vmem = pl.BlockSpec(memory_space=pltpu.VMEM)
         row = lambda t: t.reshape(1, -1)
         return pl.pallas_call(
@@ -550,6 +574,7 @@
                 pltpu.VMEM((HEADS * rows, tq), F32),
                 pltpu.VMEM((res, tq), F32),
                 pltpu.VMEM((res, tq), F32),
+                pltpu.VMEM((rows, ch, tq), F32),
                 pltpu.VMEM((xs, 2, 2 * ny, 16, 128), BF16),
                 pltpu.VMEM((xs, 2, 2 * ny, HEADS * rows, res), BF16),
                 pltpu.VMEM((xs, xs, 2, 2 * ny, HEADS * rows, tq), BF16),

time: 248 us -> 213 us (0.86)
  Pallas kernels: 242 us -> 207 us
    pallas_call x1, Pallas kernels: 242 us -> 207 us  [local(): pl.pallas_call(functools.partial(kernel, nx, ny, ck), out_shape=jax.Shape...]
where the time goes in v2:
time: 213 us; the launch traced here: 212 us
  Pallas kernels  207 us (97%)
  local copies, waits for them, and re-layouts  5.83 us (3%)
    pallas_call x1, Pallas kernels, local(): pl.pallas_call(functools.partial(kernel, nx, ny, ck), out_shape=jax.Shape...  207 us

profile of v2, /device:TPU:1, one launch (start us, length us, event | category | flops | bytes accessed | tf_op | source)
XLA Modules:
  0.0 212.5 jit_solution(10113950004372030923)
XLA Ops:
  0.0 1.4 copy.17.gb1_ref
  1.4 1.4 copy.18.gb2_ref
  2.8 206.7 %shard_map.154 = bf16[8,1024,128]{2,1,0:T(8,128)(2,1)} custom-call(bf16[8,1024,128]{2,1,0:T(8,128)(2,1)} %x_ref.1, s32[8]{0:T(128)} %mask_ref.1, f32[1,128]{1,0:T(1,128)} %bitcast.13, bf16[128,512]{1,0:T(8,128)(2,1)} %w1_ref.1, f32[128,1]{1,0:T(8,128)} %copy.17.gb1_ref, bf16[4,128]{1,0:T(4,128)(2,1)} %bitcast.9, bf16[128,128]{1,0:T(8,128)(2,1)} %ow1_ref.1, ...), custom_call_target="tpu_custom_call" | custom-call | tf_op jit(solution)/shard_map/pallas_call | solution.py:559
  209.4 3.1 %copy.20 = bf16[8,1024,128]{2,1,0:T(8,128)(2,1)} copy(bf16[8,1024,128]{2,1,0:T(8,128)(2,1)} %shard_map.154) | data formatting | bytes 4194304
